TPU v7x, 32 devices: a whole 2x2x4 slice. The times are simulated.
32 devices in a mesh: dp: 2 (over core), mp: 16 (over z, y, x).
Axes of the slice: x: 2, y: 2, z: 4, core: 2. Of those that a mesh axis runs over, the one named last changes fastest.
Arguments:
- tokens: bfloat16 [512, 2048], P('dp', 'mp'), may hold values from -6 to 6
- gate_weights: bfloat16 [2, 2048, 7168], P(None, None, 'mp'), may hold values from -0.125 to 0.125
- up_weights: bfloat16 [2, 2048, 7168], P(None, None, 'mp'), may hold values from -0.125 to 0.125
- down_weights: bfloat16 [2, 7168, 2048], P(None, 'mp'), may hold values from -0.0625 to 0.0625
- rhs_gate: float32 [2, 2048, 7168], P(None, 'dp', 'mp'), may hold values from -6 to 6
- rhs_up: float32 [2, 2048, 7168], P(None, 'dp', 'mp'), may hold values from -6 to 6
- rhs_down: float32 [2, 7168, 2048], P(None, 'mp', 'dp'), may hold values from -6 to 6
- damping: float32 [1], replicated, may hold values from 0.5 to 2
Outputs:
- step_gate: float32 [2, 2048, 7168], P(None, 'dp', 'mp')
- step_up: float32 [2, 2048, 7168], P(None, 'dp', 'mp')
- step_down: float32 [2, 7168, 2048], P(None, 'mp', 'dp')
- next_gate: float32 [2, 2048, 7168], P(None, 'dp', 'mp')
- next_up: float32 [2, 2048, 7168], P(None, 'dp', 'mp')
- next_down: float32 [2, 7168, 2048], P(None, 'mp', 'dp')
All inputs are finite; a program needn't handle non-finite values.
Results may differ from a plain program's by a relative error of at most 0.007.
Values may be sent and summed in bfloat16 or wider, within the bound.
A program may use at most 128 MiB of HBM per device.

v0:
```python
import jax
import jax.numpy as jnp
from jax import lax
from jax.sharding import PartitionSpec as P

ITERS = 1


def silu_terms(value):
    sigmoid_value = jax.nn.sigmoid(value)
    return (value * sigmoid_value, sigmoid_value * (1.0 + value * (1.0 - sigmoid_value)))


def matmul(left, right):
    return jnp.dot(left, right, preferred_element_type=jnp.float32)


def rows_product(left, right):
    return lax.dot_general(
        left, right, (((0,), (0,)), ((), ())), preferred_element_type=jnp.float32
    )


def against(left, right):
    return lax.dot_general(
        left, right, (((1,), (1,)), ((), ())), preferred_element_type=jnp.float32
    )


def local_inner(first, second):
    return (
        jnp.sum(first[0] * second[0])
        + jnp.sum(first[1] * second[1])
        + jnp.sum(first[2] * second[2])
    )


def finish_first(partial_value, whole_add):
    summed = lax.psum(partial_value, "mp")
    if whole_add is not None:
        summed = summed + whole_add.astype(jnp.float32)
    return summed.astype(jnp.bfloat16)


def body(tokens, gate_weights, up_weights, down_weights, rhs_gate, rhs_up, rhs_down, damping):
    share = tokens.shape[1]
    offset = lax.axis_index("mp") * share
    total_tokens = tokens.shape[0] * lax.axis_size("dp")
    tokens_whole = lax.all_gather(tokens, "mp", axis=1, tiled=True)
    gate_one = matmul(tokens_whole, gate_weights[0])
    up_one = matmul(tokens_whole, up_weights[0])
    active_one, slope_one = silu_terms(gate_one)
    hidden_one = (active_one * up_one).astype(jnp.bfloat16)
    layer_one = finish_first(matmul(hidden_one, down_weights[0]), tokens_whole)
    gate_two = matmul(layer_one, gate_weights[1])
    up_two = matmul(layer_one, up_weights[1])
    active_two, slope_two = silu_terms(gate_two)
    hidden_two = (active_two * up_two).astype(jnp.bfloat16)

    def curvature(vectors):
        tangent_gate, tangent_up, tangent_down = (
            lax.all_gather(vectors[0].astype(jnp.bfloat16), "dp", axis=1, tiled=True),
            lax.all_gather(vectors[1].astype(jnp.bfloat16), "dp", axis=1, tiled=True),
            lax.all_gather(vectors[2].astype(jnp.bfloat16), "dp", axis=2, tiled=True),
        )
        tan_gate = matmul(tokens_whole, tangent_gate[0])
        tan_up = matmul(tokens_whole, tangent_up[0])
        tan_hidden = (slope_one * up_one * tan_gate + active_one * tan_up).astype(jnp.bfloat16)
        tan_layer = finish_first(
            matmul(tan_hidden, down_weights[0]) + matmul(hidden_one, tangent_down[0]), None
        )
        tan_gate = matmul(tan_layer, gate_weights[1]) + matmul(layer_one, tangent_gate[1])
        tan_up = matmul(tan_layer, up_weights[1]) + matmul(layer_one, tangent_up[1])
        tan_hidden = (slope_two * up_two * tan_gate + active_two * tan_up).astype(jnp.bfloat16)
        second_partial = matmul(tan_hidden, down_weights[1]) + matmul(hidden_two, tangent_down[1])
        second_summed = lax.psum_scatter(second_partial, "mp", scatter_dimension=1, tiled=True)
        layer_slice = lax.dynamic_slice_in_dim(tan_layer, offset, share, 1)
        cotan_share = (layer_slice.astype(jnp.float32) + second_summed).astype(jnp.bfloat16)
        cotan = lax.all_gather(cotan_share, "mp", axis=1, tiled=True)
        grad_down_two = rows_product(hidden_two, cotan)
        back_hidden = against(cotan, down_weights[1])
        back_gate = (back_hidden * up_two * slope_two).astype(jnp.bfloat16)
        back_up = (back_hidden * active_two).astype(jnp.bfloat16)
        grad_gate_two = rows_product(layer_one, back_gate)
        grad_up_two = rows_product(layer_one, back_up)
        back_partial = against(back_gate, gate_weights[1]) + against(back_up, up_weights[1])
        back_layer = finish_first(back_partial, cotan)
        grad_down_one = rows_product(hidden_one, back_layer)
        back_hidden = against(back_layer, down_weights[0])
        back_gate = (back_hidden * up_one * slope_one).astype(jnp.bfloat16)
        back_up = (back_hidden * active_one).astype(jnp.bfloat16)
        grad_gate_one = rows_product(tokens_whole, back_gate)
        grad_up_one = rows_product(tokens_whole, back_up)
        summed_gate, summed_up, summed_down = (
            lax.psum_scatter(
                jnp.stack([grad_gate_one, grad_gate_two]).astype(jnp.bfloat16),
                "dp",
                scatter_dimension=1,
                tiled=True,
            ).astype(jnp.float32),
            lax.psum_scatter(
                jnp.stack([grad_up_one, grad_up_two]).astype(jnp.bfloat16),
                "dp",
                scatter_dimension=1,
                tiled=True,
            ).astype(jnp.float32),
            lax.psum_scatter(
                jnp.stack([grad_down_one, grad_down_two]).astype(jnp.bfloat16),
                "dp",
                scatter_dimension=2,
                tiled=True,
            ).astype(jnp.float32),
        )
        scale = 1.0 / total_tokens
        return (
            summed_gate * scale + damping[0] * vectors[0],
            summed_up * scale + damping[0] * vectors[1],
            summed_down * scale + damping[0] * vectors[2],
        )

    residual = (rhs_gate, rhs_up, rhs_down)
    direction = residual
    solution = (jnp.zeros_like(rhs_gate), jnp.zeros_like(rhs_up), jnp.zeros_like(rhs_down))
    norm_now = lax.psum(local_inner(residual, residual), ("dp", "mp"))
    for rounds in range(ITERS):
        image = curvature(direction)
        along, crossed, squared = lax.psum(
            (
                local_inner(direction, image),
                local_inner(residual, image),
                local_inner(image, image),
            ),
            ("dp", "mp"),
        )
        alpha = norm_now / along
        solution = tuple((solution[k] + alpha * direction[k] for k in range(3)))
        residual = tuple((residual[k] - alpha * image[k] for k in range(3)))
        norm_next = norm_now - 2.0 * alpha * crossed + alpha * alpha * squared
        direction = tuple((residual[k] + norm_next / norm_now * direction[k] for k in range(3)))
        norm_now = norm_next
    return (solution[0], solution[1], solution[2], direction[0], direction[1], direction[2])


def solution(mesh):
    in_specs = (
        P("dp", "mp"),
        P(None, None, "mp"),
        P(None, None, "mp"),
        P(None, "mp", None),
        P(None, "dp", "mp"),
        P(None, "dp", "mp"),
        P(None, "mp", "dp"),
        P(),
    )
    out_specs = (
        P(None, "dp", "mp"),
        P(None, "dp", "mp"),
        P(None, "mp", "dp"),
        P(None, "dp", "mp"),
        P(None, "dp", "mp"),
        P(None, "mp", "dp"),
    )
    return jax.shard_map(body, mesh=mesh, in_specs=in_specs, out_specs=out_specs, check_vma=False)
```

profile of v0, /device:TPU:0, one launch (start us, length us, event | category | flops | bytes accessed | tf_op | source)
XLA Modules:
  0.0 671.9 jit_solution(4627766731937684603)
XLA Ops:
  7.2 0.7 all-gather.6.cloned.1.call-update
  7.9 3.6 convert_element_type.67
  11.5 0.0 all-gather.8.cloned.1.call-start
  11.6 3.6 convert_element_type.66
  15.2 0.0 all-gather.12.cloned.1.call-start
  15.2 3.6 convert_element_type.70
  18.8 0.0 all-reduce.5.cloned.1.call-start
  18.8 46.0 %all-gather.6.cloned.1.call-done = bf16[256,2048]{1,0:T(8,128)(2,1)} async-done(((bf16[256,128]{1,0:T(8,128)(2,1)}), bf16[256,2048]{1,0:T(8,128)(2,1)}) %all-gather.6.cloned.1.call-update) | async-done | bytes 1048592 | tf_op jit(solution)/shard_map/all_gather | solution.py:49
  64.8 2.6 fusion.33
  67.4 2.4 multiply_convert_fusion.5
  69.8 0.4 copy-done.7
  70.2 2.1 fusion.27
  72.3 0.0 reduce-scatter.5.cloned.1.call-start
  72.3 6.6 all-gather.10.cloned.1.call-done
  78.9 2.2 fusion.65
  81.1 14.0 %all-gather.8.cloned.1.call-done = bf16[2,2048,448]{1,2,0:T(8,128)(2,1)} async-done(((bf16[2,1024,448]{1,2,0:T(8,128)(2,1)}), bf16[2,2048,448]{1,2,0:T(8,128)(2,1)}) %all-gather.8.cloned.1.call-update) | async-done | bytes 3670032 | tf_op jit(solution)/shard_map/all_gather | solution.py:62
  95.1 5.6 fusion.29
  100.8 10.4 %all-gather.12.cloned.1.call-done = bf16[2,448,2048]{2,1,0:T(8,128)(2,1)} async-done(((bf16[2,448,1024]{2,1,0:T(8,128)(2,1)}), bf16[2,448,2048]{2,1,0:T(8,128)(2,1)}) %all-gather.12.cloned.1.call-update) | async-done | bytes 3670032 | tf_op jit(solution)/shard_map/all_gather | solution.py:64
  111.2 2.9 convolution_add_fusion.2
  114.1 112.1 %all-reduce.8 = bf16[256,2048]{1,0:T(8,128)(2,1)} all-reduce(f32[256,2048]{1,0:T(8,128)S(1)} %convolution_add_fusion.2), channel_id=1, replica_groups=mesh['dp'=2,'mp'=16] {'mp'}, use_global_device_ids=true, to_apply=%region_4.0 | all-reduce | flops 524288 | bytes 3145728 | tf_op jit(solution)/shard_map/psum | solution.py:39
  226.1 37.1 %all-reduce.5.cloned.1.call-done = f32[256,2048]{1,0:T(8,128)} async-done(((f32[256,2048]{1,0:T(8,128)}), f32[256,2048]{1,0:T(8,128)}) %all-reduce.5.cloned.1.call-update) | async-done | bytes 2097168 | tf_op jit(solution)/shard_map/psum | solution.py:39
  263.2 2.0 add_convert_fusion.1
  265.2 0.6 copy-done.14
  265.8 0.7 fusion.23
  266.5 0.4 copy-done.16
  267.0 1.5 multiply_convert_fusion.4
  268.5 0.9 copy-done.20
  269.4 0.7 fusion.6
  270.1 1.5 fusion.60
  271.6 0.7 copy-done.21
  272.3 1.4 fusion.7
  273.8 6.2 fusion.12
  280.0 4.3 convolution_add_fusion.1
  284.3 0.0 all-gather.14.cloned.1.call-start
  284.3 80.9 %reduce-scatter.5.cloned.1.call-done = f32[256,128]{1,0:T(8,128)} async-done(((f32[256,2048]{1,0:T(8,128)}), f32[256,128]{1,0:T(8,128)}) %reduce-scatter.5.cloned.1.call-update) | async-done | bytes 131088 | tf_op jit(solution)/shard_map/reduce_scatter | solution.py:76
  365.2 1.6 add_convert_fusion.2
  366.8 49.5 %all-gather.14.cloned.1.call-done = bf16[256,2048]{1,0:T(8,128)(2,1)} async-done(((bf16[256,128]{1,0:T(8,128)(2,1)}), bf16[256,2048]{1,0:T(8,128)(2,1)}) %all-gather.14.cloned.1.call-update) | async-done | bytes 1048592 | tf_op jit(solution)/shard_map/all_gather | solution.py:79
  416.4 2.9 multiply_convert_fusion.2
  419.3 0.2 copy-done.15
  419.6 0.7 fusion.19
  420.3 1.3 copy-done.17
  421.6 2.1 convolution_add_fusion
  423.7 2.9 fusion.4
  426.6 122.9 %all-reduce.7.cloned.1.call-done = f32[256,2048]{1,0:T(8,128)} async-done(((f32[256,2048]{1,0:T(8,128)}), f32[256,2048]{1,0:T(8,128)}) %all-reduce.7.cloned.1.call-update) | async-done | bytes 2097168 | tf_op jit(solution)/shard_map/psum | solution.py:39
  549.5 3.0 fusion.25
  552.4 0.8 copy-done.6
  553.2 0.7 fusion
  554.0 2.2 pad_maximum_fusion
  556.1 0.3 reduce-scatter.9.cloned.1.call-start
  556.4 1.6 fusion.5
  558.0 1.8 fusion.1
  559.8 2.5 pad_maximum_fusion.1
  562.4 1.0 copy-done.11
  563.4 0.6 fusion.3
  564.0 2.4 fusion.2
  566.4 2.2 pad_maximum_fusion.2
  569.3 4.4 multiply_reduce_fusion.2
  573.7 9.0 %reduce-scatter.9.cloned.1.call-done = bf16[2,1024,448]{1,2,0:T(8,128)(2,1)} async-done(((bf16[2,2048,448]{1,2,0:T(8,128)(2,1)}), bf16[2,1024,448]{1,2,0:T(8,128)(2,1)}) %reduce-scatter.9.cloned.1.call-update) | async-done | bytes 1835024 | tf_op jit(solution)/shard_map/reduce_scatter | solution.py:101
  582.7 4.4 multiply_reduce_fusion.1
  588.6 10.0 %reduce-scatter.11.cloned.1.call-done = bf16[2,448,1024]{2,1,0:T(8,128)(2,1)} async-done(((bf16[2,448,2048]{2,1,0:T(8,128)(2,1)}), bf16[2,448,1024]{2,1,0:T(8,128)(2,1)}) %reduce-scatter.11.cloned.1.call-update) | async-done | bytes 1835024 | tf_op jit(solution)/shard_map/reduce_scatter | solution.py:107
  598.5 4.4 multiply_reduce_fusion
  607.4 40.6 %all-reduce = (f32[]{:T(128)}, f32[]{:T(128)}, f32[]{:T(128)}) all-reduce(f32[]{:T(128)S(6)} %add.108, f32[]{:T(128)S(6)} %add.128, f32[]{:T(128)S(6)} %add.130), channel_id=1, replica_groups=mesh['dp'=2,'mp'=16] {'dp','mp'}, use_global_device_ids=true, to_apply=%region_3.0 | all-reduce | flops 3 | bytes 24 | tf_op jit(solution)/shard_map/psum | solution.py:124
  652.0 9.2 %multiply_add_fusion.1 = (f32[2,1024,448]{1,2,0:T(8,128)}, f32[2,1024,448]{1,2,0:T(8,128)}, f32[2,1024,448]{1,2,0:T(8,128)}, f32[2,1024,448]{1,2,0:T(8,128)}) fusion(f32[2,1024,448]{1,2,0:T(8,128)} %param.13, bf16[2,1024,448]{1,2,0:T(8,128)(2,1)} %reduce-scatter.9.cloned.1.call-done, f32[]{:T(128)S(6)} %div.17, f32[]{:T(128)S(6)} %div.16, f32[]{:T(128)} %bitcast.123, ...), kind=kLoop, calls=%fused_computation.4 | loop fusion | flops 16515072 | bytes 25690124 | tf_op jit(solution)/shard_map/add | solution.py:139
  661.2 4.1 multiply_add_fusion
  (53 shorter events, 0.5 us)
Async XLA Ops:
  7.2 57.6 %all-gather.6.cloned.1.call-start = ((), (), s32[]{:S(2)}) async-start(), calls=%async_computation.4 | async-start | bytes 1114112 | tf_op jit(solution)/shard_map/all_gather | solution.py:49
  7.9 71.0 %all-gather.10.cloned.1.call-start = ((), (), s32[]{:S(2)}) async-start(), calls=%async_computation.6 | async-start | bytes 5505024 | tf_op jit(solution)/shard_map/all_gather | solution.py:63
  11.5 83.6 %all-gather.8.cloned.1.call-start = ((), (), s32[]{:S(2)}) async-start(), calls=%async_computation.5 | async-start | bytes 5505024 | tf_op jit(solution)/shard_map/all_gather | solution.py:62
  15.2 96.0 %all-gather.12.cloned.1.call-start = ((), (), s32[]{:S(2)}) async-start(), calls=%async_computation.7 | async-start | bytes 5505024 | tf_op jit(solution)/shard_map/all_gather | solution.py:64
  18.8 244.4 %all-reduce.5.cloned.1.call-start = ((), (), s32[]{:S(2)}) async-start(), calls=%async_computation.8 | async-start | bytes 4194304 | tf_op jit(solution)/shard_map/psum | solution.py:39
  64.8 2.6 copy-start.2
  67.4 27.7 %copy-start.8 = (f32[256,448]{0,1:T(8,128)}, f32[256,448]{0,1:T(8,128)S(1)}, u32[]{:S(2)}) copy-start(f32[256,448]{0,1:T(8,128)S(1)} %fusion.33) | copy-start | bytes 1376260
  67.4 2.8 copy-start.7
  69.8 25.3 %copy-start.18 = (f32[256,448]{0,1:T(8,128)}, f32[256,448]{0,1:T(8,128)S(1)}, u32[]{:S(2)}) copy-start(f32[256,448]{0,1:T(8,128)S(1)} %get-tuple-element.27) | copy-start | bytes 1376260
  72.3 293.0 %reduce-scatter.5.cloned.1.call-start = ((), (), s32[]{:S(2)}) async-start(), calls=%async_computation.9 | async-start | bytes 2228224 | tf_op jit(solution)/shard_map/reduce_scatter | solution.py:76
  263.2 2.7 copy-start.14
  263.2 3.8 copy-start.16
  267.0 3.1 copy-start.22
  267.0 2.5 copy-start.20
  267.0 3.1 copy-start.10
  270.1 2.2 copy-start.21
  284.3 132.1 %all-gather.14.cloned.1.call-start = ((), (), s32[]{:S(2)}) async-start(), calls=%async_computation.10 | async-start | bytes 1114112 | tf_op jit(solution)/shard_map/all_gather | solution.py:79
  366.8 182.6 %all-reduce.7.cloned.1.call-start = ((), (), s32[]{:S(2)}) async-start(), calls=%async_computation.11 | async-start | bytes 4194304 | tf_op jit(solution)/shard_map/psum | solution.py:39
  416.4 3.2 copy-start.15
  419.3 1.0 copy-start.12
  419.3 1.0 copy-start.13
  419.3 2.3 copy-start.17
  423.6 125.8 %copy-start.1 = (bf16[256,2048]{1,0:T(8,128)(2,1)S(1)}, bf16[256,2048]{1,0:T(8,128)(2,1)}, u32[]{:S(2)}) copy-start(bf16[256,2048]{1,0:T(8,128)(2,1)} %all-gather.14.cloned.1.call-done) | copy-start | bytes 3145732
  423.6 145.7 %reduce-scatter.7.cloned.1.call-start = ((), (), s32[]{:S(2)}) async-start(), calls=%async_computation.12 | async-start | bytes 5505024 | tf_op jit(solution)/shard_map/reduce_scatter | solution.py:95
  549.4 3.8 copy-start.9
  549.4 3.8 copy-start.19
  549.5 4.5 copy-start.4
  552.4 0.8 copy-start.6
  556.1 26.6 %reduce-scatter.9.cloned.1.call-start = ((), (), s32[]{:S(2)}) async-start(), calls=%async_computation.13 | async-start | bytes 5505024 | tf_op jit(solution)/shard_map/reduce_scatter | solution.py:101
  562.3 1.0 copy-start.11
  562.4 36.2 %reduce-scatter.11.cloned.1.call-start = ((), (), s32[]{:S(2)}) async-start(), calls=%async_computation.14 | async-start | bytes 5505024 | tf_op jit(solution)/shard_map/reduce_scatter | solution.py:107
  587.2 64.8 %copy-start.3 = (bf16[2,1024,448]{1,2,0:T(8,128)(2,1)S(1)}, bf16[2,1024,448]{1,2,0:T(8,128)(2,1)}, u32[]{:S(2)}) copy-start(bf16[2,1024,448]{1,2,0:T(8,128)(2,1)} %reduce-scatter.7.cloned.1.call-done) | copy-start | bytes 5505028
  652.0 9.2 %copy-start = (f32[2,448,1024]{2,1,0:T(8,128)S(1)}, f32[2,448,1024]{2,1,0:T(8,128)}, u32[]{:S(2)}) copy-start(f32[2,448,1024]{2,1,0:T(8,128)} %param.14) | copy-start | bytes 11010052
  652.0 9.2 %copy-start.5 = (bf16[2,448,1024]{2,1,0:T(8,128)(2,1)S(1)}, bf16[2,448,1024]{2,1,0:T(8,128)(2,1)}, u32[]{:S(2)}) copy-start(bf16[2,448,1024]{2,1,0:T(8,128)(2,1)} %reduce-scatter.11.cloned.1.call-done) | copy-start | bytes 5505028
Sparse Core Ops, SparseCore 0:
  10.7 54.0 all-gather.5
  66.9 11.8 all-gather.9
  81.0 14.0 all-gather.7
  97.1 14.0 all-gather.11
  117.1 146.0 all-reduce.4
  284.4 80.7 reduce-scatter.4
  368.5 47.8 all-gather.13
  423.8 125.6 all-reduce.6
  556.3 10.8 reduce-scatter.6
  569.8 12.9 reduce-scatter.8
  585.6 12.8 reduce-scatter.10
where the time goes:
time: 673 us; the launch traced here: 672 us
  waiting for transfers between devices  387 us (58%)
  blocking collectives  153 us (23%)
  matrix products  52.7 us (8%)
  other arithmetic  47.6 us (7%)
  between operations  24.7 us (4%)
    psum x2, waiting for transfers between devices, finish_first(): summed = lax.psum(partial_value, 'mp')  160 us
    psum x1, blocking collectives, finish_first(): summed = lax.psum(partial_value, 'mp')  112 us
    reduce_scatter x1, waiting for transfers between devices, curvature(): lax.psum_scatter(second_partial, 'mp', scatter_dimension=1, tiled=True)  80.9 us
    all_gather x1, waiting for transfers between devices, curvature(): cotan = lax.all_gather(cotan_share, 'mp', axis=1, tiled=True)  49.5 us
    all_gather x1, waiting for transfers between devices, body(): tokens_whole = lax.all_gather(tokens, 'mp', axis=1, tiled=True)  46 us
    psum x1, blocking collectives, body(): norm_now = lax.psum(local_inner(residual, residual), ('dp', 'mp'))  40.6 us
    dot_general x13, matrix products, matmul(): return jnp.dot(left, right, preferred_element_type=jnp.float32)  34 us
    all_gather x1, waiting for transfers between devices, curvature(): lax.all_gather(vectors[0].astype(jnp.bfloat16), 'dp', axis=1, tiled=True)  14 us
  transfers between devices with their start and end apart: 11, of which 10 were waited for; matrix products, arithmetic and copies ran while one was open for 8% of the time, Pallas kernels for 0%

commit v1 on v0

--- a/solution.py
+++ b/solution.py
@@ -121,7 +121,9 @@
     residual = (rhs_gate, rhs_up, rhs_down)
     direction = residual
     solution = (jnp.zeros_like(rhs_gate), jnp.zeros_like(rhs_up), jnp.zeros_like(rhs_down))
-    norm_now = lax.psum(local_inner(residual, residual), ("dp", "mp"))
+    norm_now = local_inner(residual, residual)
+    for name in ("mp", "dp"):
+        norm_now = lax.psum(norm_now, name)
     for rounds in range(ITERS):
         image = curvature(direction)
         along, crossed, squared = lax.psum(

time: 673 us -> 715 us (1.062)
  blocking collectives: 153 us -> 194 us
    psum x1 -> x3, blocking collectives: 40.6 us -> 82.4 us  [the longest x2 45.6 us: body(): norm_now = lax.psum(norm_now, name)]
  transfers between devices with their start and end apart: 11 -> 11, of which waited for: 10 -> 10; matrix products, arithmetic and copies ran while one was open for 8% -> 7% of each run, Pallas kernels for 0% -> 0%
where the time goes in v1:
time: 715 us; the launch traced here: 714 us
  waiting for transfers between devices  387 us (54%)
  blocking collectives  194 us (27%)
  matrix products  52.7 us (7%)
  other arithmetic  47.6 us (7%)
  between operations  24.7 us (3%)
    psum x2, waiting for transfers between devices, finish_first(): summed = lax.psum(partial_value, 'mp')  160 us
    psum x1, blocking collectives, finish_first(): summed = lax.psum(partial_value, 'mp')  112 us
    reduce_scatter x1, waiting for transfers between devices, curvature(): lax.psum_scatter(second_partial, 'mp', scatter_dimension=1, tiled=True)  80.9 us
    all_gather x1, waiting for transfers between devices, curvature(): cotan = lax.all_gather(cotan_share, 'mp', axis=1, tiled=True)  49.5 us
    all_gather x1, waiting for transfers between devices, body(): tokens_whole = lax.all_gather(tokens, 'mp', axis=1, tiled=True)  46 us
    psum x2, blocking collectives, body(): norm_now = lax.psum(norm_now, name)  45.6 us
    psum x1, blocking collectives, body(): lax.psum((local_inner(direction, image), local_inner(residual, image), lo...  36.8 us
    dot_general x13, matrix products, matmul(): return jnp.dot(left, right, preferred_element_type=jnp.float32)  34 us
  transfers between devices with their start and end apart: 11, of which 10 were waited for; matrix products, arithmetic and copies ran while one was open for 7% of the time, Pallas kernels for 0%

profile of v1, /device:TPU:0, one launch (start us, length us, event | category | flops | bytes accessed | tf_op | source)
XLA Modules:
  0.0 713.7 jit_solution(4923316639093777303)
XLA Ops:
  7.2 0.7 all-gather.6.cloned.1.call-update
  7.9 3.6 convert_element_type.67
  11.5 0.0 all-gather.8.cloned.1.call-start
  11.6 3.6 convert_element_type.66
  15.2 3.6 convert_element_type.70
  18.8 0.0 all-reduce.5.cloned.1.call-start
  18.8 46.0 %all-gather.6.cloned.1.call-done = bf16[256,2048]{1,0:T(8,128)(2,1)} async-done(((bf16[256,128]{1,0:T(8,128)(2,1)}), bf16[256,2048]{1,0:T(8,128)(2,1)}) %all-gather.6.cloned.1.call-update) | async-done | bytes 1048592 | tf_op jit(solution)/shard_map/all_gather | solution.py:49
  64.8 2.6 fusion.33
  67.4 2.4 multiply_convert_fusion.5
  69.8 0.4 copy-done.7
  70.2 2.1 fusion.27
  72.3 0.0 reduce-scatter.5.cloned.1.call-start
  72.3 6.6 all-gather.10.cloned.1.call-done
  78.9 2.2 fusion.65
  81.1 14.0 %all-gather.8.cloned.1.call-done = bf16[2,2048,448]{1,2,0:T(8,128)(2,1)} async-done(((bf16[2,1024,448]{1,2,0:T(8,128)(2,1)}), bf16[2,2048,448]{1,2,0:T(8,128)(2,1)}) %all-gather.8.cloned.1.call-update) | async-done | bytes 3670032 | tf_op jit(solution)/shard_map/all_gather | solution.py:62
  95.1 5.6 fusion.29
  100.8 10.4 %all-gather.12.cloned.1.call-done = bf16[2,448,2048]{2,1,0:T(8,128)(2,1)} async-done(((bf16[2,448,1024]{2,1,0:T(8,128)(2,1)}), bf16[2,448,2048]{2,1,0:T(8,128)(2,1)}) %all-gather.12.cloned.1.call-update) | async-done | bytes 3670032 | tf_op jit(solution)/shard_map/all_gather | solution.py:64
  111.2 2.9 convolution_add_fusion.2
  114.1 112.1 %all-reduce.8 = bf16[256,2048]{1,0:T(8,128)(2,1)} all-reduce(f32[256,2048]{1,0:T(8,128)S(1)} %convolution_add_fusion.2), channel_id=1, replica_groups=mesh['dp'=2,'mp'=16] {'mp'}, use_global_device_ids=true, to_apply=%region_5.0 | all-reduce | flops 524288 | bytes 3145728 | tf_op jit(solution)/shard_map/psum | solution.py:39
  226.1 37.1 %all-reduce.5.cloned.1.call-done = f32[256,2048]{1,0:T(8,128)} async-done(((f32[256,2048]{1,0:T(8,128)}), f32[256,2048]{1,0:T(8,128)}) %all-reduce.5.cloned.1.call-update) | async-done | bytes 2097168 | tf_op jit(solution)/shard_map/psum | solution.py:39
  263.2 2.0 add_convert_fusion.1
  265.2 0.6 copy-done.14
  265.8 0.7 fusion.23
  266.5 0.4 copy-done.16
  267.0 1.5 multiply_convert_fusion.4
  268.5 0.9 copy-done.20
  269.4 0.7 fusion.6
  270.1 1.5 fusion.60
  271.6 0.7 copy-done.21
  272.3 1.4 fusion.7
  273.8 6.2 fusion.12
  280.0 4.3 convolution_add_fusion.1
  284.3 80.9 %reduce-scatter.5.cloned.1.call-done = f32[256,128]{1,0:T(8,128)} async-done(((f32[256,2048]{1,0:T(8,128)}), f32[256,128]{1,0:T(8,128)}) %reduce-scatter.5.cloned.1.call-update) | async-done | bytes 131088 | tf_op jit(solution)/shard_map/reduce_scatter | solution.py:76
  365.2 1.6 add_convert_fusion.2
  366.8 49.5 %all-gather.14.cloned.1.call-done = bf16[256,2048]{1,0:T(8,128)(2,1)} async-done(((bf16[256,128]{1,0:T(8,128)(2,1)}), bf16[256,2048]{1,0:T(8,128)(2,1)}) %all-gather.14.cloned.1.call-update) | async-done | bytes 1048592 | tf_op jit(solution)/shard_map/all_gather | solution.py:79
  416.4 2.9 multiply_convert_fusion.2
  419.3 0.2 copy-done.15
  419.6 0.7 fusion.19
  420.3 1.3 copy-done.17
  421.6 2.1 convolution_add_fusion
  423.7 2.9 fusion.4
  426.6 122.9 %all-reduce.7.cloned.1.call-done = f32[256,2048]{1,0:T(8,128)} async-done(((f32[256,2048]{1,0:T(8,128)}), f32[256,2048]{1,0:T(8,128)}) %all-reduce.7.cloned.1.call-update) | async-done | bytes 2097168 | tf_op jit(solution)/shard_map/psum | solution.py:39
  549.5 3.0 fusion.25
  552.4 0.8 copy-done.6
  553.2 0.7 fusion
  554.0 2.2 pad_maximum_fusion
  556.1 0.3 reduce-scatter.9.cloned.1.call-start
  556.4 1.6 fusion.5
  558.0 1.8 fusion.1
  559.8 2.5 pad_maximum_fusion.1
  562.4 1.0 copy-done.11
  563.4 0.6 fusion.3
  564.0 2.4 fusion.2
  566.4 2.2 pad_maximum_fusion.2
  569.3 4.4 multiply_reduce_fusion.2
  573.7 9.0 %reduce-scatter.9.cloned.1.call-done = bf16[2,1024,448]{1,2,0:T(8,128)(2,1)} async-done(((bf16[2,2048,448]{1,2,0:T(8,128)(2,1)}), bf16[2,1024,448]{1,2,0:T(8,128)(2,1)}) %reduce-scatter.9.cloned.1.call-update) | async-done | bytes 1835024 | tf_op jit(solution)/shard_map/reduce_scatter | solution.py:101
  582.7 4.4 multiply_reduce_fusion.1
  588.6 9.9 %reduce-scatter.11.cloned.1.call-done = bf16[2,448,1024]{2,1,0:T(8,128)(2,1)} async-done(((bf16[2,448,2048]{2,1,0:T(8,128)(2,1)}), bf16[2,448,1024]{2,1,0:T(8,128)(2,1)}) %reduce-scatter.11.cloned.1.call-update) | async-done | bytes 1835024 | tf_op jit(solution)/shard_map/reduce_scatter | solution.py:107
  598.5 4.4 multiply_reduce_fusion
  603.6 42.6 %psum.52 = f32[]{:T(128)} all-reduce(f32[]{:T(128)S(6)} %add.110), channel_id=1, replica_groups=mesh['dp'=2,'mp'=16] {'mp'}, use_global_device_ids=true, to_apply=%region_3.0 | all-reduce | flops 1 | bytes 8 | tf_op jit(solution)/shard_map/psum | solution.py:126
  650.1 3.0 psum.53
  653.0 36.8 %all-reduce = (f32[]{:T(128)}, f32[]{:T(128)}) all-reduce(f32[]{:T(128)S(6)} %add.130, f32[]{:T(128)S(6)} %add.132), channel_id=1, replica_groups=mesh['dp'=2,'mp'=16] {'dp','mp'}, use_global_device_ids=true, to_apply=%region_15.0 | all-reduce | flops 2 | bytes 16 | tf_op jit(solution)/shard_map/psum | solution.py:129
  693.8 9.2 %multiply_add_fusion.1 = (f32[2,1024,448]{1,2,0:T(8,128)}, f32[2,1024,448]{1,2,0:T(8,128)}, f32[2,1024,448]{1,2,0:T(8,128)}, f32[2,1024,448]{1,2,0:T(8,128)}) fusion(f32[2,1024,448]{1,2,0:T(8,128)} %param.13, bf16[2,1024,448]{1,2,0:T(8,128)(2,1)} %reduce-scatter.9.cloned.1.call-done, f32[]{:T(128)S(6)} %div.17, f32[]{:T(128)S(6)} %div.16, f32[]{:T(128)} %bitcast.123, ...), kind=kLoop, calls=%fused_computation.4 | loop fusion | flops 16515072 | bytes 25690124 | tf_op jit(solution)/shard_map/add | solution.py:141
  703.0 4.1 multiply_add_fusion
  (55 shorter events, 0.6 us)
Async XLA Ops:
  7.2 57.6 %all-gather.6.cloned.1.call-start = ((), (), s32[]{:S(2)}) async-start(), calls=%async_computation.4 | async-start | bytes 1114112 | tf_op jit(solution)/shard_map/all_gather | solution.py:49
  7.9 71.0 %all-gather.10.cloned.1.call-start = ((), (), s32[]{:S(2)}) async-start(), calls=%async_computation.6 | async-start | bytes 5505024 | tf_op jit(solution)/shard_map/all_gather | solution.py:63
  11.5 83.6 %all-gather.8.cloned.1.call-start = ((), (), s32[]{:S(2)}) async-start(), calls=%async_computation.5 | async-start | bytes 5505024 | tf_op jit(solution)/shard_map/all_gather | solution.py:62
  15.2 96.0 %all-gather.12.cloned.1.call-start = ((), (), s32[]{:S(2)}) async-start(), calls=%async_computation.7 | async-start | bytes 5505024 | tf_op jit(solution)/shard_map/all_gather | solution.py:64
  18.8 244.4 %all-reduce.5.cloned.1.call-start = ((), (), s32[]{:S(2)}) async-start(), calls=%async_computation.8 | async-start | bytes 4194304 | tf_op jit(solution)/shard_map/psum | solution.py:39
  64.8 2.6 copy-start.2
  67.4 27.7 %copy-start.8 = (f32[256,448]{0,1:T(8,128)}, f32[256,448]{0,1:T(8,128)S(1)}, u32[]{:S(2)}) copy-start(f32[256,448]{0,1:T(8,128)S(1)} %fusion.33) | copy-start | bytes 1376260
  67.4 2.8 copy-start.7
  69.8 25.3 %copy-start.18 = (f32[256,448]{0,1:T(8,128)}, f32[256,448]{0,1:T(8,128)S(1)}, u32[]{:S(2)}) copy-start(f32[256,448]{0,1:T(8,128)S(1)} %get-tuple-element.26) | copy-start | bytes 1376260
  72.3 293.0 %reduce-scatter.5.cloned.1.call-start = ((), (), s32[]{:S(2)}) async-start(), calls=%async_computation.9 | async-start | bytes 2228224 | tf_op jit(solution)/shard_map/reduce_scatter | solution.py:76
  263.2 2.7 copy-start.14
  263.2 3.8 copy-start.16
  267.0 3.1 copy-start.22
  267.0 2.5 copy-start.20
  267.0 3.1 copy-start.10
  270.1 2.2 copy-start.21
  284.3 132.1 %all-gather.14.cloned.1.call-start = ((), (), s32[]{:S(2)}) async-start(), calls=%async_computation.10 | async-start | bytes 1114112 | tf_op jit(solution)/shard_map/all_gather | solution.py:79
  366.8 182.6 %all-reduce.7.cloned.1.call-start = ((), (), s32[]{:S(2)}) async-start(), calls=%async_computation.11 | async-start | bytes 4194304 | tf_op jit(solution)/shard_map/psum | solution.py:39
  416.4 3.2 copy-start.15
  419.3 1.0 copy-start.12
  419.3 1.0 copy-start.13
  419.3 2.3 copy-start.17
  423.6 125.8 %copy-start.1 = (bf16[256,2048]{1,0:T(8,128)(2,1)S(1)}, bf16[256,2048]{1,0:T(8,128)(2,1)}, u32[]{:S(2)}) copy-start(bf16[256,2048]{1,0:T(8,128)(2,1)} %all-gather.14.cloned.1.call-done) | copy-start | bytes 3145732
  423.6 145.7 %reduce-scatter.7.cloned.1.call-start = ((), (), s32[]{:S(2)}) async-start(), calls=%async_computation.12 | async-start | bytes 5505024 | tf_op jit(solution)/shard_map/reduce_scatter | solution.py:95
  549.4 3.8 copy-start.9
  549.4 3.8 copy-start.19
  549.5 4.5 copy-start.4
  552.4 0.8 copy-start.6
  556.1 26.6 %reduce-scatter.9.cloned.1.call-start = ((), (), s32[]{:S(2)}) async-start(), calls=%async_computation.13 | async-start | bytes 5505024 | tf_op jit(solution)/shard_map/reduce_scatter | solution.py:101
  562.3 1.0 copy-start.11
  562.4 36.2 %reduce-scatter.11.cloned.1.call-start = ((), (), s32[]{:S(2)}) async-start(), calls=%async_computation.14 | async-start | bytes 5505024 | tf_op jit(solution)/shard_map/reduce_scatter | solution.py:107
  587.2 106.6 %copy-start.3 = (bf16[2,1024,448]{1,2,0:T(8,128)(2,1)S(1)}, bf16[2,1024,448]{1,2,0:T(8,128)(2,1)}, u32[]{:S(2)}) copy-start(bf16[2,1024,448]{1,2,0:T(8,128)(2,1)} %reduce-scatter.7.cloned.1.call-done) | copy-start | bytes 5505028
  693.8 9.2 %copy-start = (f32[2,448,1024]{2,1,0:T(8,128)S(1)}, f32[2,448,1024]{2,1,0:T(8,128)}, u32[]{:S(2)}) copy-start(f32[2,448,1024]{2,1,0:T(8,128)} %param.14) | copy-start | bytes 11010052
  693.8 9.2 %copy-start.5 = (bf16[2,448,1024]{2,1,0:T(8,128)(2,1)S(1)}, bf16[2,448,1024]{2,1,0:T(8,128)(2,1)}, u32[]{:S(2)}) copy-start(bf16[2,448,1024]{2,1,0:T(8,128)(2,1)} %reduce-scatter.11.cloned.1.call-done) | copy-start | bytes 5505028
Sparse Core Ops, SparseCore 0:
  10.7 54.0 all-gather.5
  66.9 11.8 all-gather.9
  81.0 14.0 all-gather.7
  97.1 14.0 all-gather.11
  117.1 146.0 all-reduce.4
  284.4 80.7 reduce-scatter.4
  368.5 47.8 all-gather.13
  423.8 125.6 all-reduce.6
  556.3 10.8 reduce-scatter.6
  569.8 12.9 reduce-scatter.8
  585.6 12.8 reduce-scatter.10
